TPU v7x, 32 devices: a whole 2x2x4 slice. The times are simulated.
32 devices in a mesh: ep: 32 (over z, y, x, core).
Axes of the slice: x: 2, y: 2, z: 4, core: 2. Of those that a mesh axis runs over, the one named last changes fastest.
Arguments:
- hidden: bfloat16 [2, 1024, 3584], P(None, 'ep'), may hold values from -6 to 6
- expert_ids: int32 [2, 1024, 8], P(None, 'ep'), may hold values from 0 to 31, all different within a row; in each aligned block of 32 rows (0 to 31, 32 to 63, ..., all dimensions but the last counted through in order) at most 9 rows name the same one
- gate_scores: float32 [2, 1024, 8], P(None, 'ep'), may hold values from 0.05 to 1
- w_gate: bfloat16 [32, 3584, 1024], P('ep'), may hold values from -0.09375 to 0.09375
- w_up: bfloat16 [32, 3584, 1024], P('ep'), may hold values from -0.09375 to 0.09375
- w_down: bfloat16 [32, 1024, 3584], P('ep'), may hold values from -0.1875 to 0.1875
Outputs:
- mixed: bfloat16 [2, 1024, 3584], P(None, 'ep')
- expert_load: float32 [32], P('ep')
Inputs may be any that keep to these rules, and one draw needn't show every extreme that they name: `expert_ids`: among the 32 rows of one device in one micro-batch, no expert is named by more than 9 rows, a bound that some block reaches. Each row names 8 different experts.
All inputs are finite; a program needn't handle non-finite values.
Results may differ from a plain program's by a relative error of at most 0.004.
The roundings to bfloat16 on the way count: a program that leaves them out, or rounds other values in their place, can miss the bound.
Values may be sent and summed in bfloat16 or wider, within the bound.
A program may use at most 128 MiB of HBM per device.

v0:
```python
import jax
import jax.numpy as jnp
from jax import lax
from jax.sharding import PartitionSpec as P

route_scale = 2.5


def slot_positions(chosen_ids, experts, capacity):
    flat_ids = chosen_ids.reshape(-1)
    one_hot = (flat_ids[:, None] == jnp.arange(experts, dtype=jnp.int32)[None, :]).astype(jnp.int32)
    earlier = jnp.cumsum(one_hot, axis=0) - one_hot
    slot_index = jnp.sum(earlier * one_hot, axis=1)
    return flat_ids * capacity + slot_index


def shards(hidden, expert_ids, gate_scores, w_gate, w_up, w_down):
    devices = lax.axis_size("ep")
    exp_dev = w_gate.shape[0]
    experts = devices * exp_dev
    micro_count = hidden.shape[0]
    tok_mb = hidden.shape[1]
    model_width = hidden.shape[2]
    chosen = expert_ids.shape[2]
    capacity = tok_mb * chosen // experts + 1
    weights = route_scale * gate_scores / jnp.sum(gate_scores, axis=-1, keepdims=True)
    positions = [
        slot_positions(expert_ids[batch_index], experts, capacity)
        for batch_index in range(micro_count)
    ]
    owner = jnp.arange(tok_mb * chosen, dtype=jnp.int32) // chosen
    blank_row = jnp.zeros((1, model_width), jnp.bfloat16)

    def pack(batch_index):
        source_row = (
            jnp.full((experts * capacity,), tok_mb, jnp.int32).at[positions[batch_index]].set(owner)
        )
        padded = jnp.concatenate([hidden[batch_index], blank_row], axis=0)
        return padded[source_row].reshape(devices, exp_dev, capacity, model_width)

    def unpack(returned, batch_index):
        flat_rows = returned.reshape(experts * capacity, model_width)
        picked = (
            flat_rows[positions[batch_index]]
            .reshape(tok_mb, chosen, model_width)
            .astype(jnp.float32)
        )
        summed = jnp.sum(weights[batch_index][:, :, None] * picked, axis=1)
        return summed.astype(jnp.bfloat16)

    joined = jnp.concatenate([pack(batch_index) for batch_index in range(micro_count)], axis=2)
    block = lax.all_to_all(joined, "ep", split_axis=0, concat_axis=0, tiled=True)
    gate = jnp.einsum("nesd,edf->nesf", block, w_gate, preferred_element_type=jnp.float32)
    upper = jnp.einsum("nesd,edf->nesf", block, w_up, preferred_element_type=jnp.float32)
    hid = (jax.nn.silu(gate) * upper).astype(jnp.bfloat16)
    returned = lax.all_to_all(
        jnp.einsum("nesf,efd->nesd", hid, w_down, preferred_element_type=jnp.float32).astype(
            jnp.bfloat16
        ),
        "ep",
        split_axis=0,
        concat_axis=0,
        tiled=True,
    )
    results = [
        unpack(returned[:, :, batch_index * capacity : (batch_index + 1) * capacity], batch_index)
        for batch_index in range(micro_count)
    ]
    mixed = jnp.stack(results, axis=0)
    all_ids = expert_ids.reshape(-1)
    one_hot = (all_ids[:, None] == jnp.arange(experts, dtype=jnp.int32)[None, :]).astype(
        jnp.float32
    )
    local_term = jnp.sum(one_hot * weights.reshape(-1)[:, None], axis=0)
    summed_load = lax.psum_scatter(local_term, "ep", scatter_dimension=0, tiled=True)
    expert_load = summed_load * (experts / (route_scale * micro_count * tok_mb * devices))
    return (mixed, expert_load)


def solution(mesh):
    placed = (
        P(None, "ep", None),
        P(None, "ep", None),
        P(None, "ep", None),
        P("ep", None, None),
        P("ep", None, None),
        P("ep", None, None),
    )
    return jax.shard_map(
        shards,
        mesh=mesh,
        in_specs=placed,
        out_specs=(P(None, "ep", None), P("ep")),
        check_vma=False,
    )
```

profile of v0, /device:TPU:0, one launch (start us, length us, event | category | flops | bytes accessed | tf_op | source)
XLA Modules:
  0.0 367.0 jit_solution(14881806976863431974)
XLA Ops:
  0.6 0.7 fusion.50
  1.3 0.1 copy.43
  1.4 0.1 eq.69
  1.5 0.1 eq.65
  1.6 0.1 copy.47
  1.7 0.1 eq.77
  1.8 0.1 eq.73
  1.9 0.6 reduce-window.14
  2.5 0.2 slice_reduce_fusion.1
  2.7 0.1 copy.42
  2.8 0.1 mul.83
  2.9 0.1 fusion.41
  3.0 1.4 scatter_custom_fusion
  4.4 1.1 slice_bitcast_fusion.1
  5.5 3.1 gather_fusion
  8.6 2.7 reshape.154
  11.3 0.6 reduce-window.16
  11.9 0.2 slice_reduce_fusion
  12.1 0.1 copy.46
  12.2 0.1 mul.86
  12.3 0.1 fusion.38
  12.4 1.4 scatter_custom_fusion.1
  13.9 3.1 gather_fusion.1
  17.0 2.6 reshape.156
  19.6 4.7 %maximum_bitcast_fusion = bf16[32,1,18,3584]{3,2,1,0:T(8,128)(2,1)S(1)} fusion(bf16[32,1,9,3584]{3,2,0,1:T(8,128)(2,1)} %reshape.156, bf16[32,1,9,3584]{3,2,0,1:T(8,128)(2,1)} %reshape.154), kind=kLoop, calls=%fused_computation.14 | loop fusion | flops 8257536 | bytes 8257536 | tf_op jit(solution)/shard_map/concatenate | solution.py:51
  24.3 130.2 %all_to_all.10 = bf16[32,1,18,3584]{3,2,1,0:T(8,128)(2,1)S(1)} all-to-all(bf16[32,1,18,3584]{3,2,1,0:T(8,128)(2,1)S(1)} %maximum_bitcast_fusion), channel_id=1, replica_groups=mesh['ep'=32] {'ep'}, dimensions={0} | all-to-all | bytes 8257536 | tf_op jit(solution)/shard_map/all_to_all | solution.py:52
  154.6 0.0 copy-start
  154.6 2.4 copy-done
  157.0 6.7 %fusion.4 = f32[32,18,1024]{2,0,1:T(8,128)S(1)} fusion(bf16[1,3584,1024]{2,1,0:T(8,128)(2,1)} %param.9, bf16[32,1,18,3584]{3,2,1,0:T(8,128)(2,1)S(1)} %all_to_all.10), kind=kOutput, calls=%fused_computation.10 | convolution fusion | flops 4227858432 | bytes 13828096 | tf_op jit(solution)/shard_map/nesd,edf->nesf/dot_general | solution.py:53
  163.7 16.7 %fusion.9 = bf16[32,1,18,3584]{3,0,2,1:T(8,128)(2,1)} fusion(bf16[1,1024,3584]{2,1,0:T(8,128)(2,1)} %param.11, bf16[1,3584,1024]{2,1,0:T(8,128)(2,1)} %param.10, bf16[32,1,18,3584]{3,2,1,0:T(8,128)(2,1)} %copy-done, f32[32,18,1024]{2,0,1:T(8,128)S(1)} %fusion.4), kind=kOutput, calls=%fused_computation.13 | convolution fusion | flops 8461320192 | bytes 25296896 | tf_op jit(solution)/shard_map/nesf,efd->nesd/dot_general | solution.py:57
  180.4 6.9 %copy.52 = bf16[32,1,18,3584]{3,2,1,0:T(8,128)(2,1)} copy(bf16[32,1,18,3584]{3,0,2,1:T(8,128)(2,1)} %fusion.9) | data formatting | bytes 8257536 | tf_op jit(solution)/shard_map/convert_element_type | solution.py:57
  187.3 0.0 copy-start.1
  187.3 0.0 copy-start.2
  187.3 3.7 %all-to-all-start.1 = ((bf16[32,1,18,3584]{3,2,1,0:T(8,128)(2,1)}), bf16[32,1,18,3584]{3,2,1,0:T(8,128)(2,1)}, u32[]{:S(2)}, u32[]{:S(2)}) async-start(bf16[32,1,18,3584]{3,2,1,0:T(8,128)(2,1)} %copy.52), calls=%async_computation.1 | async-start | bytes 11010048 | tf_op jit(solution)/shard_map/all_to_all | solution.py:56
  191.1 0.0 copy-done.1
  191.1 0.1 copy.54
  191.2 0.0 copy-done.2
  191.2 0.1 copy.55
  191.3 0.1 mul.94
  191.4 0.1 eq.81
  191.5 0.1 select_reduce_fusion
  191.6 141.7 %all-reduce.2 = f32[32]{0:T(128)S(1)} all-reduce(f32[32]{0:T(128)S(1)} %select_reduce_fusion), channel_id=2, replica_groups=mesh['ep'=32] {'ep'}, use_global_device_ids=true, to_apply=%region_12.13.clone | all-reduce | flops 32 | bytes 256
  333.3 0.1 copy.41
  333.4 0.1 copy.53
  333.5 0.6 dynamic-slice
  334.7 0.0 all-to-all-done.1
  334.7 7.2 %fusion.49 = (bf16[32,1,9,3584]{3,2,1,0:T(8,128)(2,1)}, bf16[32,1,9,3584]{3,2,1,0:T(8,128)(2,1)}) fusion(bf16[32,1,18,3584]{3,2,1,0:T(8,128)(2,1)} %all-to-all-done.1), kind=kLoop, calls=%fused_computation.79 | loop fusion | bytes 8257536 | tf_op jit(solution)/shard_map/slice | solution.py:66
  341.9 4.5 %reshape.162 = bf16[288,3584]{1,0:T(8,128)(2,1)} reshape(bf16[32,1,9,3584]{3,2,1,0:T(8,128)(2,1)} %get-tuple-element.2) | data formatting | bytes 4128768 | tf_op jit(solution)/shard_map/reshape | solution.py:42
  346.4 3.2 reshape.163
  349.6 6.6 %gather_fusion.2 = bf16[256,3584]{1,0:T(8,128)(2,1)} fusion(bf16[288,3584]{1,0:T(8,128)(2,1)} %reshape.162, s32[1024]{0:T(1024)S(1)} %pad_clamp_fusion.1), kind=kCustom, calls=%fused_computation.2 | custom fusion | bytes 3671040 | tf_op jit(solution)/shard_map/gather | solution.py:44
  356.2 3.0 fusion.15
  359.1 3.0 gather_fusion.3
  362.1 3.0 fusion.14
  365.1 0.8 pad_maximum_fusion
  (20 shorter events, 0.2 us)
Async XLA Ops:
  154.6 2.4 copy-start
  187.3 3.7 %copy-start.1 = (s32[2,32,8]{1,2,0:T(8,128)S(1)}, s32[2,32,8]{1,2,0:T(8,128)}, u32[]{:S(2)}) copy-start(s32[2,32,8]{1,2,0:T(8,128)} %param.7) | copy-start | bytes 6148
  187.3 3.8 %copy-start.2 = (f32[2,32,8]{1,2,0:T(8,128)S(1)}, f32[2,32,8]{1,2,0:T(8,128)}, u32[]{:S(2)}) copy-start(f32[2,32,8]{1,2,0:T(8,128)} %param.8) | copy-start | bytes 6148
  187.3 147.4 %all-to-all-start.1 = ((bf16[32,1,18,3584]{3,2,1,0:T(8,128)(2,1)}), bf16[32,1,18,3584]{3,2,1,0:T(8,128)(2,1)}, u32[]{:S(2)}, u32[]{:S(2)}) async-start(bf16[32,1,18,3584]{3,2,1,0:T(8,128)(2,1)} %copy.52), calls=%async_computation.1 | async-start | bytes 11010048 | tf_op jit(solution)/shard_map/all_to_all | solution.py:56
where the time goes:
time: 368 us; the launch traced here: 367 us
  blocking collectives  272 us (74%)
  local copies, waits for them, and re-layouts  51.5 us (14%)
  matrix products  23.4 us (6%)
  other arithmetic  13.8 us (4%)
  starting transfers between devices  3.72 us (1%)
    unnamed x1, blocking collectives  142 us
    all_to_all x1, blocking collectives, shards(): lax.all_to_all(joined, 'ep', split_axis=0, concat_axis=0, tiled=True)  130 us
    dot_general x1, matrix products, shards(): jnp.einsum('nesf,efd->nesd', hid, w_down, preferred_element_type=jnp.floa...  16.7 us
    gather x2, local copies, waits for them, and re-layouts, unpack(): flat_rows[positions[batch_index]].reshape(tok_mb, chosen, model_width)  9.61 us
    reshape x2, local copies, waits for them, and re-layouts, unpack(): flat_rows = returned.reshape(experts * capacity, model_width)  7.64 us
  transfers between devices with their start and end apart: 1, of which 0 were waited for; matrix products, arithmetic and copies ran while one was open for 0% of the time, Pallas kernels for 0%

commit v1 on v0

v1 whole, which is shorter than its diff:
```python
import functools

import jax
import jax.numpy as jnp
from jax import lax
from jax.experimental import pallas as pl
from jax.experimental.pallas import tpu as pltpu
from jax.sharding import PartitionSpec as P

route_scale = 2.5
PLANE = 8
MESH = pl.DeviceIdType.MESH


def gather_kernel(
    planes, x_ref, g_ref, local_sem, recv_sem, core_recv, up_sem, down_sem, x_sem, y_sem, core_sem
):
    me = lax.axis_index("ep")
    p = me // PLANE
    quad = (me % PLANE) // 2
    core = me % 2
    x_quad = quad + 1 - 2 * (quad % 2)
    y_quad = (quad + 2) % 4
    d_quad = 3 - quad

    def dev(at_plane, at_quad, at_core=core):
        return at_plane * PLANE + at_quad * 2 + at_core

    up, down = me + PLANE, me - PLANE
    x_dev, y_dev, c_dev = dev(p, x_quad), dev(p, y_quad), dev(p, quad, 1 - core)

    barrier = pltpu.get_barrier_semaphore()
    for other in (x_dev, y_dev, c_dev):
        pl.semaphore_signal(barrier, inc=1, device_id=(other,), device_id_type=MESH)

    @pl.when(p < planes - 1)
    def _():
        pl.semaphore_signal(barrier, inc=1, device_id=(up,), device_id_type=MESH)

    @pl.when(p > 0)
    def _():
        pl.semaphore_signal(barrier, inc=1, device_id=(down,), device_id_type=MESH)

    below = (p + planes - 1) // planes
    above = (2 * planes - 2 - p) // planes
    pl.semaphore_wait(barrier, 3 + below + above)

    local = pltpu.make_async_copy(x_ref, g_ref.at[me], local_sem)
    local.start()

    def half(at_plane, at_quad, m, send_sem, to, own=False):
        place = g_ref.at[dev(at_plane, at_quad), m]
        return pltpu.make_async_remote_copy(
            src_ref=x_ref.at[m] if own else place,
            dst_ref=place,
            send_sem=send_sem,
            recv_sem=recv_sem.at[at_plane, at_quad, m],
            device_id=(to,),
            device_id_type=MESH,
        )

    def to_up(at_plane, m, own=False):
        return half(at_plane, quad, m, up_sem.at[at_plane, m], up, own)

    def to_down(at_plane, m, own=False):
        return half(at_plane, quad, m, down_sem.at[at_plane, m], down, own)

    def to_x(at_plane, m, own=False):
        return half(at_plane, quad, m, x_sem.at[at_plane, m], x_dev, own)

    def to_y(at_plane, m, own=False):
        return half(at_plane, quad, m, y_sem.at[at_plane, m], y_dev, own)

    def on_y(at_plane):
        return half(at_plane, x_quad, 0, y_sem.at[at_plane, 2], y_dev)

    def on_x(at_plane):
        return half(at_plane, y_quad, 1, x_sem.at[at_plane, 2], x_dev)

    def arrived(at_plane, at_quad, m):
        half(at_plane, at_quad, m, x_sem.at[at_plane, 0], x_dev).wait_recv()

    def to_core(at_plane, at_quad, own=False):
        place = g_ref.at[dev(at_plane, at_quad)]
        return pltpu.make_async_remote_copy(
            src_ref=x_ref if own else place,
            dst_ref=place,
            send_sem=core_sem.at[at_plane, at_quad],
            recv_sem=core_recv.at[at_plane, at_quad],
            device_id=(c_dev,),
            device_id_type=MESH,
        )

    def core_arrived(at_plane, at_quad):
        place = g_ref.at[dev(at_plane, at_quad, 1 - core)]
        pltpu.make_async_remote_copy(
            src_ref=place,
            dst_ref=place,
            send_sem=core_sem.at[at_plane, at_quad],
            recv_sem=core_recv.at[at_plane, at_quad],
            device_id=(c_dev,),
            device_id_type=MESH,
        ).wait_recv()

    for m in range(2):

        @pl.when(p < planes - 1)
        def _():
            to_up(p, m, True).start()

        @pl.when(p > 0)
        def _():
            to_down(p, m, True).start()

        to_x(p, m, True).start()
        to_y(p, m, True).start()
    to_core(p, quad, True).start()

    for s in range(1, planes):

        @pl.when(p >= s)
        def _():
            for m in range(2):
                arrived(p - s, quad, m)

                @pl.when(p < planes - 1)
                def _():
                    to_up(p - s, m).start()

                to_x(p - s, m).start()
                to_y(p - s, m).start()
            to_core(p - s, quad).start()

        @pl.when(p + s < planes)
        def _():
            for m in range(2):
                arrived(p + s, quad, m)

                @pl.when(p > 0)
                def _():
                    to_down(p + s, m).start()

                to_x(p + s, m).start()
                to_y(p + s, m).start()
            to_core(p + s, quad).start()

    def each(body):
        body(p)
        for s in range(1, planes):
            pl.when(p >= s)(functools.partial(body, p - s))
            pl.when(p + s < planes)(functools.partial(body, p + s))

    def across(at):
        arrived(at, x_quad, 0)
        on_y(at).start()
        arrived(at, y_quad, 0)
        arrived(at, y_quad, 1)
        on_x(at).start()
        arrived(at, x_quad, 1)
        to_core(at, x_quad).start()
        to_core(at, y_quad).start()

    def diagonal(at):
        arrived(at, d_quad, 0)
        arrived(at, d_quad, 1)
        to_core(at, d_quad).start()

    each(across)
    each(diagonal)

    def finish(at):
        for at_quad in (quad, x_quad, y_quad, d_quad):
            core_arrived(at, at_quad)
            to_core(at, at_quad).wait_send()
        for m in range(2):
            to_x(at, m).wait_send()
            to_y(at, m).wait_send()
        on_x(at).wait_send()
        on_y(at).wait_send()

    each(finish)
    for s in range(planes):

        @pl.when((p >= s) & (p < planes - 1))
        def _():
            for m in range(2):
                to_up(p - s, m).wait_send()

        @pl.when((p + s < planes) & (p > 0))
        def _():
            for m in range(2):
                to_down(p + s, m).wait_send()

    local.wait()


def gather_all(x, devices):
    planes = devices // PLANE
    dma = pltpu.SemaphoreType.DMA
    return pl.pallas_call(
        functools.partial(gather_kernel, planes),
        out_shape=jax.ShapeDtypeStruct((devices,) + x.shape, x.dtype),
        in_specs=[pl.BlockSpec(memory_space=pltpu.VMEM)],
        out_specs=pl.BlockSpec(memory_space=pl.ANY),
        scratch_shapes=[
            dma,
            dma((planes, 4, 2)),
            dma((planes, 4)),
            dma((planes, 2)),
            dma((planes, 2)),
            dma((planes, 3)),
            dma((planes, 3)),
            dma((planes, 4)),
        ],
        compiler_params=pltpu.CompilerParams(collective_id=0, has_side_effects=True),
    )(x)


def parts_of(values, count):
    parts = []
    for _ in range(count):
        part = lax.reduce_precision(values, 8, 7)
        parts.append(part.astype(jnp.bfloat16))
        values = values - part
    return parts


def ranks(mask):
    rows = mask.shape[-1]
    earlier = (jnp.arange(rows)[:, None] < jnp.arange(rows)[None, :]).astype(jnp.bfloat16)
    found = jnp.einsum(
        "...r,rt->...t", mask.astype(jnp.bfloat16), earlier, preferred_element_type=jnp.float32
    )
    return found.astype(jnp.int32)


def shards(hidden, expert_ids, gate_scores, w_gate, w_up, w_down):
    devices = lax.axis_size("ep")
    planes = devices // PLANE
    me = lax.axis_index("ep")
    my_plane, my_place = me // PLANE, me % PLANE
    micro_count, tok_mb, model_width = hidden.shape
    chosen = expert_ids.shape[2]
    capacity = tok_mb * chosen // devices + 1
    weights = route_scale * gate_scores / jnp.sum(gate_scores, axis=-1, keepdims=True)

    extra = jnp.concatenate([expert_ids.astype(jnp.bfloat16)] + parts_of(weights, 3), axis=-1)
    extra = jnp.pad(extra, ((0, 0), (0, 0), (0, 128 - extra.shape[-1])))
    everyone = gather_all(jnp.concatenate([hidden, extra], axis=-1), devices)

    notes = everyone[..., model_width:].astype(jnp.float32)
    all_ids = notes[..., :chosen].astype(jnp.int32)
    all_weights = (
        notes[..., chosen : 2 * chosen]
        + notes[..., 2 * chosen : 3 * chosen]
        + notes[..., 3 * chosen : 4 * chosen]
    )
    named = all_ids == me
    expert_load = jnp.sum(jnp.where(named, all_weights, 0.0)).reshape(1) * (
        devices / (route_scale * micro_count * tok_mb * devices)
    )

    mask = jnp.any(named, axis=-1)
    slots = jnp.arange(capacity, dtype=jnp.int32)
    hit = mask[:, :, None, :] & (ranks(mask)[:, :, None, :] == slots[:, None])
    row_at = jnp.sum(jnp.where(hit, jnp.arange(tok_mb, dtype=jnp.int32), 0), axis=-1)
    block_at = jnp.arange(devices * micro_count, dtype=jnp.int32).reshape(devices, micro_count, 1)
    row_at = (row_at + block_at * tok_mb).reshape(planes, PLANE, micro_count * capacity)
    row_at = row_at.transpose(1, 0, 2).reshape(-1)

    table = everyone.reshape(devices * micro_count * tok_mb, -1)
    rows = jnp.take(table, row_at, axis=0, mode="clip")[:, :model_width]
    gate = jnp.dot(rows, w_gate[0], preferred_element_type=jnp.float32)
    upper = jnp.dot(rows, w_up[0], preferred_element_type=jnp.float32)
    hid = (jax.nn.silu(gate) * upper).astype(jnp.bfloat16)
    answer = jnp.dot(hid, w_down[0], preferred_element_type=jnp.float32).astype(jnp.bfloat16)

    in_plane = [[k * PLANE + i for i in range(PLANE)] for k in range(planes)]
    in_column = [[k * PLANE + i for k in range(planes)] for i in range(PLANE)]
    returned = lax.all_to_all(
        answer.reshape(PLANE, -1, model_width),
        "ep",
        split_axis=0,
        concat_axis=0,
        tiled=True,
        axis_index_groups=in_plane,
    ).reshape(-1, model_width)

    column = (planes, PLANE) + all_ids.shape[1:]
    ids = lax.dynamic_index_in_dim(all_ids.reshape(column), my_place, 1, keepdims=False)
    share = lax.dynamic_index_in_dim(all_weights.reshape(column), my_place, 1, keepdims=False)
    experts_here = my_plane * PLANE + jnp.arange(PLANE, dtype=jnp.int32)
    same = ids[:, :, None] == experts_here[:, None, None]
    here = jnp.any(same, axis=-1)
    weight_here = jnp.sum(jnp.where(same, share[:, :, None], 0.0), axis=-1)
    spots = here[..., None] & (ranks(here)[..., None] == slots)
    spread = jnp.where(spots, weight_here[..., None], 0.0)
    spread = spread.transpose(0, 1, 3, 2, 4).reshape(planes * micro_count, tok_mb, PLANE, 1, capacity)
    diag = jnp.eye(planes * micro_count, dtype=jnp.float32)[:, None, None, :, None]
    matrix = (spread * diag).reshape(planes * micro_count * tok_mb, -1)
    partial = sum(
        jnp.dot(part, returned, preferred_element_type=jnp.float32) for part in parts_of(matrix, 2)
    ).astype(jnp.bfloat16)
    swapped = lax.all_to_all(
        partial.reshape(planes, micro_count * tok_mb, model_width),
        "ep",
        split_axis=0,
        concat_axis=0,
        tiled=True,
        axis_index_groups=in_column,
    )
    mixed = jnp.sum(swapped.astype(jnp.float32), axis=0).astype(jnp.bfloat16)
    return (mixed.reshape(micro_count, tok_mb, model_width), expert_load)


def solution(mesh):
    placed = (
        P(None, "ep", None),
        P(None, "ep", None),
        P(None, "ep", None),
        P("ep", None, None),
        P("ep", None, None),
        P("ep", None, None),
    )
    return jax.shard_map(
        shards,
        mesh=mesh,
        in_specs=placed,
        out_specs=(P(None, "ep", None), P("ep")),
        check_vma=False,
    )
```

time: 368 us -> 234 us (0.64)
  blocking collectives: 272 us -> 0 us
  waiting for transfers between devices: 0.01 us -> 84.1 us
  Pallas kernels: 0 us -> 70 us
  local copies, waits for them, and re-layouts: 51.5 us -> 21.1 us
  matrix products: 23.4 us -> 35.8 us
  starting transfers between devices: 3.72 us -> 9.54 us
  other arithmetic: 13.8 us -> 9.88 us
    unnamed x1 -> x0, blocking collectives: 142 us -> none
    all_to_all x1 -> x0, blocking collectives: 130 us -> none  [shards(): lax.all_to_all(joined, 'ep', split_axis=0, concat_axis=0, tiled=True)]
    all_to_all x1 -> x2, waiting for transfers between devices: 0.01 us -> 84.1 us  [the longest x1 45.1 us: shards(): lax.all_to_all(answer.reshape(PLANE, -1, model_width), 'ep', split_axis=0...]
    pallas_call x0 -> x1, Pallas kernels: none -> 70 us  [gather_all(): pl.pallas_call(functools.partial(gather_kernel, planes), out_shape=jax.Sh...]
    reshape x4 -> x0, local copies, waits for them, and re-layouts: 12.9 us -> none  [the longest x2 7.64 us: unpack(): flat_rows = returned.reshape(experts * capacity, model_width)]
    dot_general x2 -> x6, matrix products: 23.4 us -> 35.8 us  [the longest x1 16.5 us: shards(): jnp.dot(hid, w_down[0], preferred_element_type=jnp.float32)]
    slice x4 -> x0, local copies, waits for them, and re-layouts: 7.51 us -> none  [the longest x1 7.18 us: shards(): returned[:, :, batch_index * capacity:(batch_index + 1) * capacity]]
    all_to_all x1 -> x2, starting transfers between devices: 3.72 us -> 9.54 us  [the longest x1 4.79 us: shards(): lax.all_to_all(partial.reshape(planes, micro_count * tok_mb, model_width)...]
  transfers between devices with their start and end apart: 1 -> 2, of which waited for: 0 -> 2; matrix products, arithmetic and copies ran while one was open for 0% -> 1% of each run, Pallas kernels for 0% -> 0%
where the time goes in v1:
time: 234 us; the launch traced here: 233 us
  waiting for transfers between devices  84.1 us (36%)
  Pallas kernels  70 us (30%)
  matrix products  35.8 us (15%)
  local copies, waits for them, and re-layouts  21.1 us (9%)
  other arithmetic  9.88 us (4%)
  starting transfers between devices  9.54 us (4%)
  between operations  2.62 us (1%)
    pallas_call x1, Pallas kernels, gather_all(): pl.pallas_call(functools.partial(gather_kernel, planes), out_shape=jax.Sh...  70 us
    all_to_all x1, waiting for transfers between devices, shards(): lax.all_to_all(answer.reshape(PLANE, -1, model_width), 'ep', split_axis=0...  45.1 us
    all_to_all x1, waiting for transfers between devices, shards(): lax.all_to_all(partial.reshape(planes, micro_count * tok_mb, model_width)...  39 us
    gather x1, local copies, waits for them, and re-layouts, shards(): rows = jnp.take(table, row_at, axis=0, mode='clip')[:, :model_width]  18.1 us
    dot_general x1, matrix products, shards(): jnp.dot(hid, w_down[0], preferred_element_type=jnp.float32)  16.5 us
    dot_general x1, matrix products, shards(): gate = jnp.dot(rows, w_gate[0], preferred_element_type=jnp.float32)  10.2 us
    dot_general x2, matrix products, shards(): jnp.dot(part, returned, preferred_element_type=jnp.float32)  8.94 us
    all_to_all x1, starting transfers between devices, shards(): lax.all_to_all(partial.reshape(planes, micro_count * tok_mb, model_width)...  4.79 us
  transfers between devices with their start and end apart: 2, of which 2 were waited for; matrix products, arithmetic and copies ran while one was open for 1% of the time, Pallas kernels for 0%

profile of v1, /device:TPU:0, one launch (start us, length us, event | category | flops | bytes accessed | tf_op | source)
XLA Modules:
  0.0 233.1 jit_solution(12924472928605485564)
XLA Ops:
  0.6 0.8 copy.48
  1.4 0.7 reduce_sum.48
  2.1 0.7 convert_element_type.76
  2.8 0.1 copy.50
  2.9 0.1 reduce-precision_convert_fusion.2
  3.0 0.1 fusion.35
  3.1 1.8 pad_maximum_fusion.x_ref
  5.0 70.0 %shard_map.77 = bf16[32,2,32,3712]{3,2,1,0:T(8,128)(2,1)} custom-call(bf16[2,32,3712]{2,1,0:T(8,128)(2,1)} %pad_maximum_fusion.x_ref), custom_call_target="tpu_custom_call" | custom-call | tf_op jit(solution)/shard_map/pallas_call | solution.py:200
  74.9 1.2 slice_convert_fusion.1
  76.1 1.5 select_reduce_fusion
  77.6 1.2 reduce_or.19
  78.8 0.1 convolution_convert_fusion
  78.9 0.4 select_reduce_fusion.1
  79.3 0.1 reshape.128
  79.4 0.1 copy.61
  79.5 0.1 reshape.119
  79.7 18.1 %gather_fusion = bf16[576,3712]{1,0:T(8,128)(2,1)} fusion(bf16[2048,3712]{1,0:T(8,128)(2,1)} %bitcast.59, s32[1024]{0:T(1024)S(1)} %pad_clamp_fusion), kind=kCustom, calls=%fused_computation | custom fusion | bytes 8554752 | tf_op jit(solution)/shard_map/jit(_take)/gather | solution.py:272
  97.8 10.2 %fusion.4 = f32[576,1024]{1,0:T(8,128)} fusion(bf16[1,3584,1024]{2,1,0:T(8,128)(2,1)} %param.9, bf16[576,3712]{1,0:T(8,128)(2,1)} %gather_fusion), kind=kOutput, calls=%fused_computation.5 | convolution fusion | flops 4227858432 | bytes 13828096 | tf_op jit(solution)/shard_map/dot_general | solution.py:273
  108.0 16.5 %fusion.6 = bf16[576,3584]{1,0:T(8,128)(2,1)} fusion(bf16[1,1024,3584]{2,1,0:T(8,128)(2,1)} %param.11, f32[576,1024]{1,0:T(8,128)} %fusion.4, bf16[1,3584,1024]{2,1,0:T(8,128)(2,1)} %param.10, bf16[576,3712]{1,0:T(8,128)(2,1)} %gather_fusion), kind=kOutput, calls=%fused_computation.7 | convolution fusion | flops 8461320192 | bytes 25296896 | tf_op jit(solution)/shard_map/dot_general | solution.py:276
  124.4 4.8 %all-to-all-start = ((bf16[8,72,3584]{2,1,0:T(8,128)(2,1)}), bf16[8,72,3584]{2,1,0:T(8,128)(2,1)}, u32[]{:S(2)}, u32[]{:S(2)}) async-start(bf16[8,72,3584]{2,1,0:T(8,128)(2,1)} %bitcast.60), calls=%async_computation | async-start | bytes 8257536 | tf_op jit(solution)/shard_map/all_to_all | solution.py:280
  129.3 0.1 copy.62
  129.4 0.1 copy.63
  129.4 0.2 fusion.26
  129.6 0.2 compare_reduce_fusion
  129.8 0.1 convolution_convert_fusion.1
  130.0 0.1 fusion.24
  130.0 0.6 fusion.13
  130.7 0.8 convert_element_type.91
  131.5 0.8 convert_element_type.86
  132.3 45.1 %all-to-all-done = bf16[8,72,3584]{2,1,0:T(8,128)(2,1)} async-done(((bf16[8,72,3584]{2,1,0:T(8,128)(2,1)}), bf16[8,72,3584]{2,1,0:T(8,128)(2,1)}, u32[]{:S(2)}, u32[]{:S(2)}) %all-to-all-start) | async-done | bytes 4128800 | tf_op jit(solution)/shard_map/all_to_all | solution.py:280
  177.4 3.8 %fusion.42 = f32[256,3584]{1,0:T(8,128)S(1)} fusion(bf16[256,576]{0,1:T(8,128)(2,1)S(1)} %convert_element_type.86, bf16[576,3584]{1,0:T(8,128)(2,1)} %bitcast.19), kind=kOutput, calls=%fused_computation.63 | convolution fusion | flops 1056964608 | bytes 8093696 | tf_op jit(solution)/shard_map/dot_general | solution.py:302
  181.2 5.1 %fusion.9 = bf16[256,3584]{1,0:T(8,128)(2,1)} fusion(f32[256,3584]{1,0:T(8,128)S(1)} %fusion.42, bf16[256,576]{0,1:T(8,128)(2,1)S(1)} %convert_element_type.91, bf16[576,3584]{1,0:T(8,128)(2,1)} %bitcast.19), kind=kOutput, calls=%fused_computation.9 | convolution fusion | flops 1058799616 | bytes 9928704 | tf_op jit(solution)/shard_map/dot_general | solution.py:302
  186.3 4.8 %all-to-all-start.1 = ((bf16[4,64,3584]{2,1,0:T(8,128)(2,1)}), bf16[4,64,3584]{2,1,0:T(8,128)(2,1)S(1)}, u32[]{:S(2)}, u32[]{:S(2)}) async-start(bf16[4,64,3584]{2,1,0:T(8,128)(2,1)} %bitcast.20), calls=%async_computation.1 | async-start | bytes 3670016 | tf_op jit(solution)/shard_map/all_to_all | solution.py:304
  191.8 39.0 %all-to-all-done.1 = bf16[4,64,3584]{2,1,0:T(8,128)(2,1)S(1)} async-done(((bf16[4,64,3584]{2,1,0:T(8,128)(2,1)}), bf16[4,64,3584]{2,1,0:T(8,128)(2,1)S(1)}, u32[]{:S(2)}, u32[]{:S(2)}) %all-to-all-start.1) | async-done | bytes 1835040 | tf_op jit(solution)/shard_map/all_to_all | solution.py:304
  230.8 1.1 reduce_sum.51
  (12 shorter events, 0.1 us)
Async XLA Ops:
  124.4 52.9 %all-to-all-start = ((bf16[8,72,3584]{2,1,0:T(8,128)(2,1)}), bf16[8,72,3584]{2,1,0:T(8,128)(2,1)}, u32[]{:S(2)}, u32[]{:S(2)}) async-start(bf16[8,72,3584]{2,1,0:T(8,128)(2,1)} %bitcast.60), calls=%async_computation | async-start | bytes 8257536 | tf_op jit(solution)/shard_map/all_to_all | solution.py:280
  186.3 44.5 %all-to-all-start.1 = ((bf16[4,64,3584]{2,1,0:T(8,128)(2,1)}), bf16[4,64,3584]{2,1,0:T(8,128)(2,1)S(1)}, u32[]{:S(2)}, u32[]{:S(2)}) async-start(bf16[4,64,3584]{2,1,0:T(8,128)(2,1)} %bitcast.20), calls=%async_computation.1 | async-start | bytes 3670016 | tf_op jit(solution)/shard_map/all_to_all | solution.py:304

commit v2 on v1

--- a/solution.py
+++ b/solution.py
@@ -216,6 +216,155 @@
     )(x)
 
 
+def return_kernel(
+    planes, hid_ref, down_ref, matrix_ref, out_ref, w_buf, answers, inbox, sums, column, w_sem, a_send, a_recv, s_send, s_recv
+):
+    me = lax.axis_index("ep")
+    p = me // PLANE
+    q = me % PLANE
+    chunks, depth, width = w_buf.shape
+
+    def load(c):
+        place = pl.multiple_of(c * width, width)
+        return pltpu.make_async_copy(
+            down_ref.at[:, pl.ds(place, width)], w_buf.at[c], w_sem.at[c]
+        )
+
+    for c in range(chunks):
+        load(c).start()
+
+    barrier = pltpu.get_barrier_semaphore()
+    for i in range(1, PLANE):
+        other = p * PLANE + (q + i) % PLANE
+        pl.semaphore_signal(barrier, inc=1, device_id=(other,), device_id_type=MESH)
+    for i in range(1, planes):
+        other = ((p + i) % planes) * PLANE + q
+        pl.semaphore_signal(barrier, inc=1, device_id=(other,), device_id_type=MESH)
+    pl.semaphore_wait(barrier, PLANE + planes - 2)
+
+    def answer_copy(c, i):
+        place = (q + i) % PLANE
+        return pltpu.make_async_remote_copy(
+            src_ref=answers.at[c, place],
+            dst_ref=inbox.at[c, q],
+            send_sem=a_send.at[c, i],
+            recv_sem=a_recv.at[c, q],
+            device_id=(p * PLANE + place,),
+            device_id_type=MESH,
+        )
+
+    def answer_arrived(c, i):
+        place = (q + i) % PLANE
+        pltpu.make_async_remote_copy(
+            src_ref=answers.at[c, place],
+            dst_ref=inbox.at[c, place],
+            send_sem=a_send.at[c, i],
+            recv_sem=a_recv.at[c, place],
+            device_id=(p * PLANE + place,),
+            device_id_type=MESH,
+        ).wait_recv()
+
+    def sum_copy(c, i):
+        place = (p + i) % planes
+        return pltpu.make_async_remote_copy(
+            src_ref=sums.at[c, place],
+            dst_ref=column.at[c, p],
+            send_sem=s_send.at[c, i],
+            recv_sem=s_recv.at[c, p],
+            device_id=(place * PLANE + q,),
+            device_id_type=MESH,
+        )
+
+    def sum_arrived(c, i):
+        place = (p + i) % planes
+        pltpu.make_async_remote_copy(
+            src_ref=sums.at[c, place],
+            dst_ref=column.at[c, place],
+            send_sem=s_send.at[c, i],
+            recv_sem=s_recv.at[c, place],
+            device_id=(place * PLANE + q,),
+            device_id_type=MESH,
+        ).wait_recv()
+
+    def compute(c, carry):
+        load(c).wait()
+        found = jnp.dot(hid_ref[...], w_buf[c], preferred_element_type=jnp.float32)
+        answers[c] = found.reshape(answers.shape[1:]).astype(jnp.bfloat16)
+        for i in range(1, PLANE):
+            answer_copy(c, i).start()
+        inbox[c, q] = answers[c, q]
+        return carry
+
+    lax.fori_loop(0, chunks, compute, 0)
+
+    def combine(c, carry):
+        for i in range(1, PLANE):
+            answer_arrived(c, i)
+        total = jnp.zeros((matrix_ref.shape[2], width), jnp.float32)
+        for k in range(PLANE):
+            for half in range(2):
+                total += jnp.dot(
+                    matrix_ref[k, half], inbox[c, k], preferred_element_type=jnp.float32
+                )
+        sums[c] = total.reshape(sums.shape[1:]).astype(jnp.bfloat16)
+        for i in range(1, planes):
+            sum_copy(c, i).start()
+        column[c, p] = sums[c, p]
+        return carry
+
+    lax.fori_loop(0, chunks, combine, 0)
+
+    def gather_sums(c, carry):
+        for i in range(1, planes):
+            sum_arrived(c, i)
+        total = column[c, 0].astype(jnp.float32)
+        for k in range(1, planes):
+            total += column[c, k].astype(jnp.float32)
+        out_ref[c] = total.astype(jnp.bfloat16)
+        return carry
+
+    lax.fori_loop(0, chunks, gather_sums, 0)
+
+    def finish(c, carry):
+        for i in range(1, PLANE):
+            answer_copy(c, i).wait_send()
+        for i in range(1, planes):
+            sum_copy(c, i).wait_send()
+        return carry
+
+    lax.fori_loop(0, chunks, finish, 0)
+
+
+def return_all(hid, w_down, matrix, devices):
+    planes = devices // PLANE
+    depth, model_width = w_down.shape
+    width = next(w for w in (512, 256, 128) if model_width % w == 0)
+    chunks = model_width // width
+    rows = hid.shape[0] // PLANE
+    tokens = matrix.shape[2] // planes
+    dma = pltpu.SemaphoreType.DMA
+    vmem = pl.BlockSpec(memory_space=pltpu.VMEM)
+    return pl.pallas_call(
+        functools.partial(return_kernel, planes),
+        out_shape=jax.ShapeDtypeStruct((chunks, tokens, width), jnp.bfloat16),
+        in_specs=[vmem, pl.BlockSpec(memory_space=pl.ANY), vmem],
+        out_specs=vmem,
+        scratch_shapes=[
+            pltpu.VMEM((chunks, depth, width), jnp.bfloat16),
+            pltpu.VMEM((chunks, PLANE, rows, width), jnp.bfloat16),
+            pltpu.VMEM((chunks, PLANE, rows, width), jnp.bfloat16),
+            pltpu.VMEM((chunks, planes, tokens, width), jnp.bfloat16),
+            pltpu.VMEM((chunks, planes, tokens, width), jnp.bfloat16),
+            dma((chunks,)),
+            dma((chunks, PLANE)),
+            dma((chunks, PLANE)),
+            dma((chunks, planes)),
+            dma((chunks, planes)),
+        ],
+        compiler_params=pltpu.CompilerParams(collective_id=1, has_side_effects=True),
+    )(hid, w_down, matrix)
+
+
 def parts_of(values, count):
     parts = []
     for _ in range(count):
@@ -273,18 +422,6 @@
     gate = jnp.dot(rows, w_gate[0], preferred_element_type=jnp.float32)
     upper = jnp.dot(rows, w_up[0], preferred_element_type=jnp.float32)
     hid = (jax.nn.silu(gate) * upper).astype(jnp.bfloat16)
-    answer = jnp.dot(hid, w_down[0], preferred_element_type=jnp.float32).astype(jnp.bfloat16)
-
-    in_plane = [[k * PLANE + i for i in range(PLANE)] for k in range(planes)]
-    in_column = [[k * PLANE + i for k in range(planes)] for i in range(PLANE)]
-    returned = lax.all_to_all(
-        answer.reshape(PLANE, -1, model_width),
-        "ep",
-        split_axis=0,
-        concat_axis=0,
-        tiled=True,
-        axis_index_groups=in_plane,
-    ).reshape(-1, model_width)
 
     column = (planes, PLANE) + all_ids.shape[1:]
     ids = lax.dynamic_index_in_dim(all_ids.reshape(column), my_place, 1, keepdims=False)
@@ -295,21 +432,13 @@
     weight_here = jnp.sum(jnp.where(same, share[:, :, None], 0.0), axis=-1)
     spots = here[..., None] & (ranks(here)[..., None] == slots)
     spread = jnp.where(spots, weight_here[..., None], 0.0)
-    spread = spread.transpose(0, 1, 3, 2, 4).reshape(planes * micro_count, tok_mb, PLANE, 1, capacity)
-    diag = jnp.eye(planes * micro_count, dtype=jnp.float32)[:, None, None, :, None]
-    matrix = (spread * diag).reshape(planes * micro_count * tok_mb, -1)
-    partial = sum(
-        jnp.dot(part, returned, preferred_element_type=jnp.float32) for part in parts_of(matrix, 2)
-    ).astype(jnp.bfloat16)
-    swapped = lax.all_to_all(
-        partial.reshape(planes, micro_count * tok_mb, model_width),
-        "ep",
-        split_axis=0,
-        concat_axis=0,
-        tiled=True,
-        axis_index_groups=in_column,
-    )
-    mixed = jnp.sum(swapped.astype(jnp.float32), axis=0).astype(jnp.bfloat16)
+    groups = planes * micro_count
+    spread = spread.transpose(2, 0, 1, 3, 4).reshape(PLANE, groups, tok_mb, 1, capacity)
+    diag = jnp.eye(groups, dtype=jnp.float32)[:, None, :, None]
+    matrix = (spread * diag).reshape(PLANE, groups * tok_mb, groups * capacity)
+    matrix = jnp.stack(parts_of(matrix, 2), axis=1)
+    mixed = return_all(hid, w_down[0], matrix, devices)
+    mixed = mixed.transpose(1, 0, 2)
     return (mixed.reshape(micro_count, tok_mb, model_width), expert_load)
 
 

time: 234 us -> 183 us (0.78)
  waiting for transfers between devices: 84.1 us -> 0 us
  Pallas kernels: 70 us -> 132 us
  matrix products: 35.8 us -> 14.5 us
  starting transfers between devices: 9.54 us -> 0 us
  local copies, waits for them, and re-layouts: 21.1 us -> 23.5 us
    all_to_all x2 -> x0, waiting for transfers between devices: 84.1 us -> none  [the longest x1 45.1 us: shards(): lax.all_to_all(answer.reshape(PLANE, -1, model_width), 'ep', split_axis=0...]
    pallas_call x0 -> x1, Pallas kernels: none -> 61.8 us  [return_all(): pl.pallas_call(functools.partial(return_kernel, planes), out_shape=jax.Sh...]
    dot_general x3 -> x1, matrix products: 25.4 us -> 5.62 us  [shards(): upper = jnp.dot(rows, w_up[0], preferred_element_type=jnp.float32)]
    all_to_all x2 -> x0, starting transfers between devices: 9.54 us -> none  [the longest x1 4.79 us: shards(): lax.all_to_all(partial.reshape(planes, micro_count * tok_mb, model_width)...]
  transfers between devices with their start and end apart: 2 -> 0, of which waited for: 2 -> 0; matrix products, arithmetic and copies ran while one was open for 1% -> 0% of each run, Pallas kernels for 0% -> 0%
where the time goes in v2:
time: 183 us; the launch traced here: 182 us
  Pallas kernels  132 us (72%)
  local copies, waits for them, and re-layouts  23.5 us (13%)
  matrix products  14.5 us (8%)
  other arithmetic  9.62 us (5%)
  between operations  2.7 us (1%)
    pallas_call x1, Pallas kernels, gather_all(): pl.pallas_call(functools.partial(gather_kernel, planes), out_shape=jax.Sh...  70 us
    pallas_call x1, Pallas kernels, return_all(): pl.pallas_call(functools.partial(return_kernel, planes), out_shape=jax.Sh...  61.8 us
    gather x1, local copies, waits for them, and re-layouts, shards(): rows = jnp.take(table, row_at, axis=0, mode='clip')[:, :model_width]  18.1 us
    dot_general x1, matrix products, shards(): gate = jnp.dot(rows, w_gate[0], preferred_element_type=jnp.float32)  8.66 us
    dot_general x1, matrix products, shards(): upper = jnp.dot(rows, w_up[0], preferred_element_type=jnp.float32)  5.62 us

profile of v2, /device:TPU:0, one launch (start us, length us, event | category | flops | bytes accessed | tf_op | source)
XLA Modules:
  0.0 182.1 jit_solution(17652441174464936461)
XLA Ops:
  0.7 0.7 reduce_sum.36
  1.4 0.7 convert_element_type.64
  2.1 0.1 copy.62
  2.2 0.8 copy.60
  3.0 0.1 reduce-precision_convert_fusion.2
  3.1 0.1 fusion.24
  3.2 0.1 mul.73
  3.2 0.1 mul.74
  3.4 1.8 %pad_maximum_fusion.1.x_ref = bf16[2,32,3712]{2,1,0:T(8,128)(2,1)} fusion(bf16[2,32,128]{2,1,0:T(8,128)(2,1)S(1)} %fusion.24, bf16[2,32,3584]{2,1,0:T(8,128)(2,1)} %param.6), kind=kLoop, calls=%fused_computation.22 | loop fusion | flops 950272 | bytes 950272 | tf_op jit(solution)/shard_map/concatenate | solution.py:398
  5.2 70.0 %shard_map.77 = bf16[32,2,32,3712]{3,2,1,0:T(8,128)(2,1)} custom-call(bf16[2,32,3712]{2,1,0:T(8,128)(2,1)} %pad_maximum_fusion.1.x_ref), custom_call_target="tpu_custom_call" | custom-call | tf_op jit(solution)/shard_map/pallas_call | solution.py:200
  75.2 1.2 slice_convert_fusion.1
  76.4 1.5 select_reduce_fusion
  78.5 0.1 copy.78
  78.6 0.1 copy.79
  78.7 0.2 fusion.15
  78.9 0.2 compare_reduce_fusion
  79.1 1.2 reduce_or.18
  80.3 0.1 convolution_convert_fusion.1
  80.4 0.4 select_reduce_fusion.1
  80.9 0.1 reshape.125
  80.9 0.1 copy.77
  81.1 0.1 reshape.116
  81.2 18.1 %gather_fusion = bf16[576,3712]{1,0:T(8,128)(2,1)} fusion(bf16[2048,3712]{1,0:T(8,128)(2,1)} %bitcast.48, s32[1024]{0:T(1024)S(1)} %pad_clamp_fusion), kind=kCustom, calls=%fused_computation | custom fusion | bytes 8554752 | tf_op jit(solution)/shard_map/jit(_take)/gather | solution.py:421
  99.3 0.1 convolution_convert_fusion
  99.4 0.1 fusion.14
  99.5 0.2 mul.71
  99.7 0.7 mul.72
  100.3 0.1 bitcast_multiply_fusion
  100.4 0.3 copy.73
  100.7 0.2 reduce-precision_convert_fusion
  101.0 0.0 slice-start
  101.0 0.0 slice-start.2
  101.0 1.2 pad_maximum_fusion.matrix_ref
  102.2 0.0 slice-start.1
  102.2 0.0 slice-start.3
  102.2 8.7 %fusion.2 = f32[576,1024]{1,0:T(8,128)S(1)} fusion(bf16[1,3584,1024]{2,1,0:T(8,128)(2,1)} %param.9, bf16[576,3712]{1,0:T(8,128)(2,1)} %gather_fusion), kind=kOutput, calls=%fused_computation.3 | convolution fusion | flops 4227858432 | bytes 13828096 | tf_op jit(solution)/shard_map/dot_general | solution.py:422
  110.9 0.0 slice-done
  110.9 0.0 slice-done.2
  110.9 0.0 slice-done.1
  110.9 0.0 slice-done.3
  111.0 5.6 %multiply_convert_fusion.hid_ref = bf16[576,1024]{1,0:T(8,128)(2,1)} fusion(f32[576,1024]{1,0:T(8,128)S(1)} %fusion.2, bf16[1,3584,1024]{2,1,0:T(8,128)(2,1)S(1)} %bitcast.63, bf16[576,3712]{1,0:T(8,128)(2,1)S(1)} %bitcast.51), kind=kOutput, calls=%fused_computation.7 | convolution fusion | flops 4231397376 | bytes 15007744 | tf_op jit(solution)/shard_map/dot_general | solution.py:423
  116.6 61.8 %shard_map.78 = bf16[7,64,512]{2,1,0:T(8,128)(2,1)} custom-call(bf16[576,1024]{1,0:T(8,128)(2,1)} %multiply_convert_fusion.hid_ref, bf16[1024,3584]{1,0:T(8,128)(2,1)} %bitcast.49, bf16[8,2,256,72]{3,2,1,0:T(8,128)(2,1)} %pad_maximum_fusion.matrix_ref), custom_call_target="tpu_custom_call" | custom-call | tf_op jit(solution)/shard_map/pallas_call | solution.py:347
  178.4 1.3 copy.75
  179.6 1.3 reshape.113
  (14 shorter events, 0.1 us)
Async XLA Ops:
  101.0 9.9 %slice-start = ((s8[4276224]{0:T(1024)(128)(4,1)}), s8[4194304]{0:T(1024)(128)(4,1)S(1)}, s32[]{:S(2)}) async-start(s8[4276224]{0:T(1024)(128)(4,1)} %bitcast.50), calls=%async_computation | async-start | bytes 8388608
  101.0 9.9 %slice-start.2 = ((s8[7340032]{0:T(1024)(128)(4,1)}), s8[4194304]{0:T(1024)(128)(4,1)S(1)}, s32[]{:S(2)}) async-start(s8[7340032]{0:T(1024)(128)(4,1)} %bitcast.62), calls=%async_computation.2 | async-start | bytes 8388608
  102.2 8.7 %slice-start.1 = ((s8[4276224]{0:T(1024)(128)(4,1)}), s8[81920]{0:T(1024)(128)(4,1)S(1)}, s32[]{:S(2)}) async-start(s8[4276224]{0:T(1024)(128)(4,1)} %bitcast.50), calls=%async_computation.1 | async-start | bytes 163840
  102.2 8.7 %slice-start.3 = ((s8[7340032]{0:T(1024)(128)(4,1)}), s8[3145728]{0:T(1024)(128)(4,1)S(1)}, s32[]{:S(2)}) async-start(s8[7340032]{0:T(1024)(128)(4,1)} %bitcast.62), calls=%async_computation.3 | async-start | bytes 6291456

commit v3 on v2

--- a/solution.py
+++ b/solution.py
@@ -13,7 +13,23 @@
 
 
 def gather_kernel(
-    planes, x_ref, g_ref, local_sem, recv_sem, core_recv, up_sem, down_sem, x_sem, y_sem, core_sem
+    planes,
+    capacity,
+    chosen,
+    x_ref,
+    g_ref,
+    rows_ref,
+    notes_ref,
+    table,
+    local_sem,
+    recv_sem,
+    core_recv,
+    up_sem,
+    down_sem,
+    x_sem,
+    y_sem,
+    core_sem,
+    table_sem,
 ):
     me = lax.axis_index("ep")
     p = me // PLANE
@@ -26,6 +42,9 @@
     def dev(at_plane, at_quad, at_core=core):
         return at_plane * PLANE + at_quad * 2 + at_core
 
+    def block(at_plane, at_quad, at_core=core):
+        return g_ref.at[at_quad * 2 + at_core, at_plane]
+
     up, down = me + PLANE, me - PLANE
     x_dev, y_dev, c_dev = dev(p, x_quad), dev(p, y_quad), dev(p, quad, 1 - core)
 
@@ -45,11 +64,11 @@
     above = (2 * planes - 2 - p) // planes
     pl.semaphore_wait(barrier, 3 + below + above)
 
-    local = pltpu.make_async_copy(x_ref, g_ref.at[me], local_sem)
+    local = pltpu.make_async_copy(x_ref, block(p, quad), local_sem)
     local.start()
 
     def half(at_plane, at_quad, m, send_sem, to, own=False):
-        place = g_ref.at[dev(at_plane, at_quad), m]
+        place = block(at_plane, at_quad).at[m]
         return pltpu.make_async_remote_copy(
             src_ref=x_ref.at[m] if own else place,
             dst_ref=place,
@@ -81,7 +100,7 @@
         half(at_plane, at_quad, m, x_sem.at[at_plane, 0], x_dev).wait_recv()
 
     def to_core(at_plane, at_quad, own=False):
-        place = g_ref.at[dev(at_plane, at_quad)]
+        place = block(at_plane, at_quad)
         return pltpu.make_async_remote_copy(
             src_ref=x_ref if own else place,
             dst_ref=place,
@@ -92,7 +111,7 @@
         )
 
     def core_arrived(at_plane, at_quad):
-        place = g_ref.at[dev(at_plane, at_quad, 1 - core)]
+        place = block(at_plane, at_quad, 1 - core)
         pltpu.make_async_remote_copy(
             src_ref=place,
             dst_ref=place,
@@ -165,12 +184,69 @@
         arrived(at, d_quad, 1)
         to_core(at, d_quad).start()
 
+    local.wait()
+
+    tok_mb, wide = x_ref.shape[1:]
+    depth = planes * 2 * tok_mb
+    model_width = rows_ref.shape[2]
+    token = lax.broadcasted_iota(jnp.int32, (depth, depth), 0)
+    other = lax.broadcasted_iota(jnp.int32, (depth, depth), 1)
+    before = (other < token) & (lax.div(other, tok_mb) == lax.div(token, tok_mb))
+    before = jnp.where(before, 1.0, 0.0).astype(jnp.bfloat16)
+    lanes = (depth, 128)
+    start = lax.div(lax.broadcasted_iota(jnp.int32, lanes, 0), tok_mb) * capacity
+    lane = lax.broadcasted_iota(jnp.int32, lanes, 1)
+
+    def fetch(place, slot):
+        return pltpu.make_async_copy(g_ref.at[place], table.at[slot], table_sem.at[slot])
+
+    def select(place, slot):
+        fetch(place, slot).wait()
+        notes = table[slot, :, :, :, model_width:]
+        notes_ref[place] = notes
+        ids = notes.reshape(lanes).astype(jnp.float32).astype(jnp.int32)
+        named = jnp.where((ids == me) & (lane < chosen), 1.0, 0.0)
+        named = jnp.broadcast_to(jnp.sum(named, axis=1, keepdims=True), lanes)
+        rank = jnp.dot(before, named.astype(jnp.bfloat16), preferred_element_type=jnp.float32)
+        spot = start + rank.astype(jnp.int32)
+        pick = jnp.where((lane == spot) & (named > 0.5), 1.0, 0.0).astype(jnp.bfloat16)
+        found = lax.dot_general(
+            pick,
+            table[slot, :, :, :, :model_width].reshape(depth, model_width),
+            (((0,), (0,)), ((), ())),
+            preferred_element_type=jnp.float32,
+        )
+        rows_ref[place] = found[: rows_ref.shape[1]].astype(jnp.bfloat16)
+
     each(across)
+
+    def others(at_quad):
+        each(lambda at: core_arrived(at, at_quad))
+
+    fetch(quad * 2 + core, 0).start()
+    fetch(x_quad * 2 + core, 1).start()
+    select(quad * 2 + core, 0)
+    fetch(y_quad * 2 + core, 0).start()
+    select(x_quad * 2 + core, 1)
+    others(quad)
+    fetch(quad * 2 + 1 - core, 1).start()
+    select(y_quad * 2 + core, 0)
+    others(x_quad)
+    fetch(x_quad * 2 + 1 - core, 0).start()
+    select(quad * 2 + 1 - core, 1)
     each(diagonal)
+    fetch(d_quad * 2 + core, 1).start()
+    select(x_quad * 2 + 1 - core, 0)
+    others(y_quad)
+    fetch(y_quad * 2 + 1 - core, 0).start()
+    select(d_quad * 2 + core, 1)
+    others(d_quad)
+    fetch(d_quad * 2 + 1 - core, 1).start()
+    select(y_quad * 2 + 1 - core, 0)
+    select(d_quad * 2 + 1 - core, 1)
 
     def finish(at):
         for at_quad in (quad, x_quad, y_quad, d_quad):
-            core_arrived(at, at_quad)
             to_core(at, at_quad).wait_send()
         for m in range(2):
             to_x(at, m).wait_send()
@@ -191,18 +267,25 @@
             for m in range(2):
                 to_down(p + s, m).wait_send()
 
-    local.wait()
-
-
-def gather_all(x, devices):
+
+def gather_all(x, model_width, capacity, chosen, devices):
     planes = devices // PLANE
     dma = pltpu.SemaphoreType.DMA
     return pl.pallas_call(
-        functools.partial(gather_kernel, planes),
-        out_shape=jax.ShapeDtypeStruct((devices,) + x.shape, x.dtype),
+        functools.partial(gather_kernel, planes, capacity, chosen),
+        out_shape=(
+            jax.ShapeDtypeStruct((PLANE, planes) + x.shape, x.dtype),
+            jax.ShapeDtypeStruct((PLANE, planes * 2 * capacity, model_width), x.dtype),
+            jax.ShapeDtypeStruct((PLANE, planes) + x.shape[:2] + (128,), x.dtype),
+        ),
         in_specs=[pl.BlockSpec(memory_space=pltpu.VMEM)],
-        out_specs=pl.BlockSpec(memory_space=pl.ANY),
+        out_specs=(
+            pl.BlockSpec(memory_space=pl.ANY),
+            pl.BlockSpec(memory_space=pltpu.VMEM),
+            pl.BlockSpec(memory_space=pltpu.VMEM),
+        ),
         scratch_shapes=[
+            pltpu.VMEM((2, planes) + x.shape, x.dtype),
             dma,
             dma((planes, 4, 2)),
             dma((planes, 4)),
@@ -211,6 +294,7 @@
             dma((planes, 3)),
             dma((planes, 3)),
             dma((planes, 4)),
+            dma((2,)),
         ],
         compiler_params=pltpu.CompilerParams(collective_id=0, has_side_effects=True),
     )(x)
@@ -395,9 +479,11 @@
 
     extra = jnp.concatenate([expert_ids.astype(jnp.bfloat16)] + parts_of(weights, 3), axis=-1)
     extra = jnp.pad(extra, ((0, 0), (0, 0), (0, 128 - extra.shape[-1])))
-    everyone = gather_all(jnp.concatenate([hidden, extra], axis=-1), devices)
-
-    notes = everyone[..., model_width:].astype(jnp.float32)
+    _, rows, notes = gather_all(
+        jnp.concatenate([hidden, extra], axis=-1), model_width, capacity, chosen, devices
+    )
+    rows = rows.reshape(-1, model_width)
+    notes = notes.astype(jnp.float32)
     all_ids = notes[..., :chosen].astype(jnp.int32)
     all_weights = (
         notes[..., chosen : 2 * chosen]
@@ -409,23 +495,13 @@
         devices / (route_scale * micro_count * tok_mb * devices)
     )
 
-    mask = jnp.any(named, axis=-1)
     slots = jnp.arange(capacity, dtype=jnp.int32)
-    hit = mask[:, :, None, :] & (ranks(mask)[:, :, None, :] == slots[:, None])
-    row_at = jnp.sum(jnp.where(hit, jnp.arange(tok_mb, dtype=jnp.int32), 0), axis=-1)
-    block_at = jnp.arange(devices * micro_count, dtype=jnp.int32).reshape(devices, micro_count, 1)
-    row_at = (row_at + block_at * tok_mb).reshape(planes, PLANE, micro_count * capacity)
-    row_at = row_at.transpose(1, 0, 2).reshape(-1)
-
-    table = everyone.reshape(devices * micro_count * tok_mb, -1)
-    rows = jnp.take(table, row_at, axis=0, mode="clip")[:, :model_width]
     gate = jnp.dot(rows, w_gate[0], preferred_element_type=jnp.float32)
     upper = jnp.dot(rows, w_up[0], preferred_element_type=jnp.float32)
     hid = (jax.nn.silu(gate) * upper).astype(jnp.bfloat16)
 
-    column = (planes, PLANE) + all_ids.shape[1:]
-    ids = lax.dynamic_index_in_dim(all_ids.reshape(column), my_place, 1, keepdims=False)
-    share = lax.dynamic_index_in_dim(all_weights.reshape(column), my_place, 1, keepdims=False)
+    ids = lax.dynamic_index_in_dim(all_ids, my_place, 0, keepdims=False)
+    share = lax.dynamic_index_in_dim(all_weights, my_place, 0, keepdims=False)
     experts_here = my_plane * PLANE + jnp.arange(PLANE, dtype=jnp.int32)
     same = ids[:, :, None] == experts_here[:, None, None]
     here = jnp.any(same, axis=-1)

time: 183 us -> 170 us (0.929)
  local copies, waits for them, and re-layouts: 23.5 us -> 5.05 us
  Pallas kernels: 132 us -> 137 us
  matrix products: 14.5 us -> 18 us
  other arithmetic: 9.62 us -> 6.94 us
    gather x1 -> x0, local copies, waits for them, and re-layouts: 18.1 us -> none  [shards(): rows = jnp.take(table, row_at, axis=0, mode='clip')[:, :model_width]]
    pallas_call x1, Pallas kernels: 70 us -> 75 us  [gather_all(): pl.pallas_call(functools.partial(gather_kernel, planes, capacity, chosen)...]
    dot_general x1, matrix products: 5.62 us -> 8.89 us  [shards(): upper = jnp.dot(rows, w_up[0], preferred_element_type=jnp.float32)]
where the time goes in v3:
time: 170 us; the launch traced here: 169 us
  Pallas kernels  137 us (81%)
  matrix products  18 us (11%)
  other arithmetic  6.94 us (4%)
  local copies, waits for them, and re-layouts  5.05 us (3%)
  between operations  2.59 us (2%)
    pallas_call x1, Pallas kernels, gather_all(): pl.pallas_call(functools.partial(gather_kernel, planes, capacity, chosen)...  75 us
    pallas_call x1, Pallas kernels, return_all(): pl.pallas_call(functools.partial(return_kernel, planes), out_shape=jax.Sh...  61.8 us
    dot_general x1, matrix products, shards(): gate = jnp.dot(rows, w_gate[0], preferred_element_type=jnp.float32)  8.94 us
    dot_general x1, matrix products, shards(): upper = jnp.dot(rows, w_up[0], preferred_element_type=jnp.float32)  8.89 us

profile of v3, /device:TPU:0, one launch (start us, length us, event | category | flops | bytes accessed | tf_op | source)
XLA Modules:
  0.0 169.3 jit_solution(1572744591920512166)
XLA Ops:
  0.6 0.7 reduce_sum.27
  1.3 0.8 copy.37
  2.1 0.1 reduce-precision_convert_fusion.2
  2.2 0.7 convert_element_type.59
  2.9 0.1 copy.39
  3.0 0.1 fusion.19
  3.1 1.8 %pad_maximum_fusion.1.x_ref = bf16[2,32,3712]{2,1,0:T(8,128)(2,1)} fusion(bf16[2,32,128]{2,1,0:T(8,128)(2,1)S(1)} %fusion.19, bf16[2,32,3584]{2,1,0:T(8,128)(2,1)} %param.6), kind=kLoop, calls=%fused_computation.16 | loop fusion | flops 950272 | bytes 950272 | tf_op jit(solution)/shard_map/concatenate | solution.py:483
  4.9 75.0 %shard_map.77 = (bf16[8,4,2,32,3712]{4,3,2,1,0:T(8,128)(2,1)}, bf16[8,72,3584]{2,1,0:T(8,128)(2,1)}, bf16[8,4,2,32,128]{4,3,2,1,0:T(8,128)(2,1)}) custom-call(bf16[2,32,3712]{2,1,0:T(8,128)(2,1)} %pad_maximum_fusion.1.x_ref), custom_call_target="tpu_custom_call" | custom-call | tf_op jit(solution)/shard_map/pallas_call | solution.py:274
  79.9 0.0 copy-start.1
  79.9 8.9 %fusion.2 = f32[576,1024]{1,0:T(8,128)S(1)} fusion(bf16[576,3584]{1,0:T(8,128)(2,1)} %bitcast.49, bf16[1,3584,1024]{2,1,0:T(8,128)(2,1)} %param.9), kind=kOutput, calls=%fused_computation.2 | convolution fusion | flops 4227858432 | bytes 13828096 | tf_op jit(solution)/shard_map/dot_general | solution.py:499
  88.9 0.0 copy-done.1
  88.9 0.0 copy-start
  88.9 8.9 %multiply_convert_fusion.hid_ref = bf16[576,1024]{1,0:T(8,128)(2,1)} fusion(f32[576,1024]{1,0:T(8,128)S(1)} %fusion.2, bf16[576,3584]{1,0:T(8,128)(2,1)S(1)} %bitcast.50, bf16[1,3584,1024]{2,1,0:T(8,128)(2,1)} %param.10), kind=kOutput, calls=%fused_computation.4 | convolution fusion | flops 4231397376 | bytes 15007744 | tf_op jit(solution)/shard_map/dot_general | solution.py:500
  97.8 0.0 copy-done
  97.8 0.1 convert_element_type.64
  97.9 1.5 select_reduce_fusion
  99.4 0.1 copy.43
  99.5 0.1 copy.40
  99.6 0.2 fusion.10
  99.8 0.2 compare_reduce_fusion
  100.0 0.1 convolution_convert_fusion
  100.1 0.1 fusion.9
  100.2 0.2 mul.58
  100.3 0.7 mul.59
  101.0 0.1 mul.60
  101.1 0.1 mul.61
  101.3 0.3 copy.46
  101.6 0.2 reduce-precision_convert_fusion
  101.9 1.2 pad_maximum_fusion.matrix_ref
  103.1 61.8 %shard_map.78 = bf16[7,64,512]{2,1,0:T(8,128)(2,1)} custom-call(bf16[576,1024]{1,0:T(8,128)(2,1)} %multiply_convert_fusion.hid_ref, bf16[1024,3584]{1,0:T(8,128)(2,1)} %bitcast.41, bf16[8,2,256,72]{3,2,1,0:T(8,128)(2,1)} %pad_maximum_fusion.matrix_ref), custom_call_target="tpu_custom_call" | custom-call | tf_op jit(solution)/shard_map/pallas_call | solution.py:431
  164.9 1.3 copy.48
  166.2 1.3 reshape.75
  (8 shorter events, 0.1 us)
Async XLA Ops:
  79.9 9.0 %copy-start.1 = (bf16[8,72,3584]{2,1,0:T(8,128)(2,1)S(1)}, bf16[8,72,3584]{2,1,0:T(8,128)(2,1)}, u32[]{:S(2)}) copy-start(bf16[8,72,3584]{2,1,0:T(8,128)(2,1)} %get-tuple-element.4) | copy-start | bytes 12386308
  88.9 8.9 %copy-start = (bf16[8,4,2,32,128]{4,3,2,1,0:T(8,128)(2,1)S(1)}, bf16[8,4,2,32,128]{4,3,2,1,0:T(8,128)(2,1)}, u32[]{:S(2)}) copy-start(bf16[8,4,2,32,128]{4,3,2,1,0:T(8,128)(2,1)} %get-tuple-element.5) | copy-start | bytes 1572868
